TPU v7x, 32 devices: a whole 2x2x4 slice. The times are simulated.
32 devices in a mesh: groups: 1, expert: 16 (over z, y, x), replica: 2 (over core).
Axes of the slice: x: 2, y: 2, z: 4, core: 2. Of those that a mesh axis runs over, the one named last changes fastest.
Arguments:
- queries: bfloat16 [128, 8192], P(('groups', 'expert', 'replica')), may hold values from -250 to 250
- token_keys: bfloat16 [128, 512], P(('groups', 'expert', 'replica')), may hold values from -6 to 6
- token_values: bfloat16 [128, 512], P(('groups', 'expert', 'replica')), may hold values from -6 to 6
- stored_keys: bfloat16 [128, 256, 512], P(('groups', 'expert', 'replica')), may hold values from -7 to 7
- stored_values: bfloat16 [128, 256, 512], P(('groups', 'expert', 'replica')), may hold values from -6 to 6
- kv_len: int32 [128], P(('groups', 'expert', 'replica')), may hold values from 2 to 256, as said below
- residual: bfloat16 [128, 4096], P(('groups', 'expert', 'replica')), may hold values from -6 to 6
- out_weight: bfloat16 [8192, 4096], P(('expert', 'replica')), may hold values from -0.1875 to 0.1875
- norm_gain: bfloat16 [4096], replicated, may hold values from 0.25 to 1.75
- expert_ids: int32 [128, 8], P(('groups', 'expert')), may hold values from 0 to 15, all different within a row; in each aligned block of 8 rows (0 to 7, 8 to 15, ...) at most 4 rows name the same one
- route_weight: float32 [128, 8], P(('groups', 'expert')), may hold values from 0.05 to 1
- w_gate: bfloat16 [16, 4096, 768], P('expert', None, 'replica'), may hold values from -0.09375 to 0.09375
- w_up: bfloat16 [16, 4096, 768], P('expert', None, 'replica'), may hold values from -0.09375 to 0.09375
- w_down: bfloat16 [16, 768, 4096], P('expert', 'replica'), may hold values from -0.4375 to 0.4375
Outputs:
- updated: bfloat16 [128, 4096], P(('groups', 'expert', 'replica'))
Inputs may be any that keep to these rules, and one draw needn't show every extreme that they name: `kv_len`: at least 2; some sequence uses all 256 positions. `expert_ids`: each token names 8 different experts; in each aligned block of 8 tokens no expert is named by more than 4 tokens, and some block reaches it.
All inputs are finite; a program needn't handle non-finite values.
Results may differ from a plain program's by a relative error of at most 0.01.
Values may be sent and summed in bfloat16 or wider, within the bound.
A program may use at most 64 MiB of HBM per device.

v0:
```python
import math
import jax
import jax.numpy as jnp
from jax import lax
from jax.sharding import PartitionSpec as P

HEAD_WIDTH = 128


def shifted(block, axis, distance):
    devices = range(lax.axis_size(axis))
    route = [(i - distance, i) for i in devices if i - distance in devices]
    return lax.ppermute(block, axis, route)


def attend_local(queries, token_keys, token_values, stored_keys, stored_values, kv_len):
    seq_count = queries.shape[0]
    cache_len = stored_keys.shape[1]
    kv_count = token_keys.shape[1] // HEAD_WIDTH
    query_group_width = queries.shape[1] // HEAD_WIDTH // kv_count
    query_head_rows = queries.reshape(seq_count, kv_count, query_group_width, HEAD_WIDTH)
    keys_from_cache = stored_keys.reshape(seq_count, cache_len, kv_count, HEAD_WIDTH)
    values_from_cache = stored_values.reshape(seq_count, cache_len, kv_count, HEAD_WIDTH)
    keys_latest = token_keys.reshape(seq_count, kv_count, HEAD_WIDTH)
    values_latest = token_values.astype(jnp.float32).reshape(seq_count, kv_count, HEAD_WIDTH)
    inv_root = 1.0 / math.sqrt(HEAD_WIDTH)
    cached_scores = (
        jnp.einsum(
            "bgqd,bpgd->bgqp", query_head_rows, keys_from_cache, preferred_element_type=jnp.float32
        )
        * inv_root
    )
    positions = lax.broadcasted_iota(jnp.int32, (seq_count, cache_len), 1)
    visible = positions < kv_len[:, None]
    cached_scores = jnp.where(visible[:, None, None, :], cached_scores, -jnp.inf)
    fresh_score = (
        jnp.einsum(
            "bgqd,bgd->bgq", query_head_rows, keys_latest, preferred_element_type=jnp.float32
        )
        * inv_root
    )
    highest = jnp.maximum(jnp.max(cached_scores, axis=-1), fresh_score)
    cached_exp = jnp.exp(cached_scores - highest[..., None])
    fresh_exp = jnp.exp(fresh_score - highest)
    totals = jnp.sum(cached_exp, axis=-1) + fresh_exp
    cached_prob = (cached_exp / totals[..., None]).astype(jnp.bfloat16)
    fresh_prob = lax.optimization_barrier((fresh_exp / totals).astype(jnp.bfloat16)).astype(
        jnp.float32
    )
    mixed = jnp.einsum(
        "bgqp,bpgd->bgqd", cached_prob, values_from_cache, preferred_element_type=jnp.float32
    )
    mixed = mixed + fresh_prob[..., None] * values_latest[:, :, None, :]
    return mixed.reshape(seq_count, -1).astype(jnp.bfloat16)


def on_device(
    queries,
    token_keys,
    token_values,
    stored_keys,
    stored_values,
    kv_len,
    residual,
    out_weight,
    norm_gain,
    expert_ids,
    route_weight,
    w_gate,
    w_up,
    w_down,
):
    attended = attend_local(queries, token_keys, token_values, stored_keys, stored_values, kv_len)
    column_groups = 8
    device_count = lax.axis_size(("expert", "replica"))
    seq_count, feature_total = attended.shape
    row_count, model_width = out_weight.shape
    feature_groups = device_count // column_groups
    feature_block = feature_total // feature_groups
    col_width = model_width // column_groups
    device_rank = lax.axis_index(("expert", "replica"))
    block_place = device_rank % column_groups
    slot_ids = jnp.arange(column_groups, dtype=jnp.int32)
    own_piece = lax.dynamic_slice_in_dim(out_weight, block_place * col_width, col_width, 1)
    empty_block = jnp.zeros((column_groups, row_count, col_width), out_weight.dtype)
    stacked = jnp.where((slot_ids == block_place)[:, None, None], own_piece[None], empty_block)
    for offset in range(1 - column_groups, column_groups):
        if offset != 0:
            target_place = (device_rank + offset) % column_groups
            sent_piece = lax.dynamic_slice_in_dim(
                out_weight, target_place * col_width, col_width, 1
            )
            arrived_piece = shifted(sent_piece, ("expert", "replica"), offset)
            stacked = jnp.where(
                (slot_ids == block_place - offset)[:, None, None], arrived_piece[None], stacked
            )
    weight_block = stacked.reshape(column_groups * row_count, col_width)
    repeated = jnp.repeat(
        attended.reshape(seq_count, feature_groups, feature_block), column_groups, axis=1
    )
    all_tokens = lax.all_to_all(
        repeated, ("expert", "replica"), split_axis=1, concat_axis=0, tiled=True
    )
    all_tokens = all_tokens.reshape(-1, feature_block)
    partial_cols = jnp.dot(all_tokens, weight_block, preferred_element_type=jnp.float32)
    partial_cols = partial_cols.reshape(-1, 1, col_width)
    came_back = lax.all_to_all(
        partial_cols.astype(jnp.bfloat16),
        ("expert", "replica"),
        split_axis=0,
        concat_axis=1,
        tiled=True,
    ).astype(partial_cols.dtype)
    projected = jnp.sum(
        came_back.reshape(seq_count, feature_groups, column_groups, col_width), axis=1
    ).reshape(seq_count, model_width)
    hidden_state = residual.astype(jnp.float32) + projected
    mean_square = jnp.mean(hidden_state * hidden_state, axis=-1, keepdims=True)
    normed = (hidden_state * lax.rsqrt(mean_square + 1e-06) * norm_gain.astype(jnp.float32)).astype(
        jnp.bfloat16
    )
    pair_tokens = lax.all_gather(normed, "replica", axis=0, tiled=True)
    token_count, topk_count = expert_ids.shape
    expert_count = lax.axis_size("expert")
    capacity = max(2, -(-(token_count * topk_count) // expert_count))
    flat_ids = expert_ids.reshape(-1)
    row_total = flat_ids.shape[0]
    same_expert = flat_ids[:, None] == flat_ids[None, :]
    row_iota = lax.broadcasted_iota(jnp.int32, (row_total, row_total), 0)
    col_iota = lax.broadcasted_iota(jnp.int32, (row_total, row_total), 1)
    slot_ranks = jnp.sum(jnp.where(same_expert & (col_iota < row_iota), 1, 0), axis=1).astype(
        jnp.int32
    )
    slot_of = (flat_ids * capacity + slot_ranks).reshape(token_count, topk_count)
    slot_total = expert_count * capacity
    slot_iota = jnp.arange(slot_total, dtype=jnp.int32)
    slot_hits = slot_of[None, :, :] == slot_iota[:, None, None]
    pick_table = jnp.sum(slot_hits.astype(jnp.float32), axis=2).astype(jnp.bfloat16)
    outgoing = jnp.dot(pick_table, pair_tokens, preferred_element_type=jnp.float32).astype(
        jnp.bfloat16
    )
    outgoing = outgoing.reshape(expert_count, capacity, -1)
    mixing = route_weight / jnp.sum(route_weight, axis=1, keepdims=True)
    combine_rows = jnp.sum(jnp.where(slot_hits, mixing[None, :, :], 0.0), axis=2).T
    incoming = lax.all_to_all(outgoing, "expert", split_axis=0, concat_axis=0, tiled=True)
    model_width = incoming.shape[-1]
    lead_shape = incoming.shape[:2]
    slot_rows = incoming.reshape(-1, model_width)
    gate_act = jnp.dot(slot_rows, w_gate[0], preferred_element_type=jnp.float32)
    up_act = jnp.dot(slot_rows, w_up[0], preferred_element_type=jnp.float32)
    hidden_act = (jax.nn.silu(gate_act) * up_act).astype(jnp.bfloat16)
    partial_value = jnp.dot(hidden_act, w_down[0], preferred_element_type=jnp.float32).reshape(
        lead_shape + (model_width,)
    )
    summed_halves = lax.psum(partial_value.astype(jnp.bfloat16), "replica").astype(jnp.float32)
    arrived = lax.all_to_all(
        summed_halves.astype(jnp.bfloat16), "expert", split_axis=0, concat_axis=0, tiled=True
    ).astype(summed_halves.dtype)
    returned = arrived
    returned = returned.reshape(slot_total, -1)
    seq_count = normed.shape[0]
    own_rows = lax.dynamic_slice_in_dim(
        combine_rows, lax.axis_index("replica") * seq_count, seq_count, 0
    )
    moe_out = jnp.dot(
        own_rows, returned, precision=lax.Precision.HIGHEST, preferred_element_type=jnp.float32
    )
    return (hidden_state + moe_out).astype(jnp.bfloat16)


def solution(mesh):
    in_specs = (
        P(("groups", "expert", "replica"), None),
        P(("groups", "expert", "replica"), None),
        P(("groups", "expert", "replica"), None),
        P(("groups", "expert", "replica"), None, None),
        P(("groups", "expert", "replica"), None, None),
        P(("groups", "expert", "replica")),
        P(("groups", "expert", "replica"), None),
        P(("expert", "replica"), None),
        P(),
        P(("groups", "expert"), None),
        P(("groups", "expert"), None),
        P("expert", None, "replica"),
        P("expert", None, "replica"),
        P("expert", "replica", None),
    )
    out_specs = P(("groups", "expert", "replica"), None)
    return jax.shard_map(
        on_device, mesh=mesh, in_specs=in_specs, out_specs=out_specs, check_vma=False
    )
```

profile of v0, /device:TPU:0, one launch (start us, length us, event | category | flops | bytes accessed | tf_op | source)
XLA Modules:
  0.0 200.0 jit_solution(9605539332392520658)
XLA Ops:
  6.6 4.1 %constant_dynamic-slice_fusion.15 = (bf16[256,512]{1,0:T(8,128)(2,1)}, bf16[256,512]{1,0:T(8,128)(2,1)}, bf16[256,512]{1,0:T(8,128)(2,1)}, bf16[256,512]{1,0:T(8...) fusion(bf16[256,4096]{1,0:T(8,128)(2,1)} %param.21, ...), kind=kLoop, calls=%fused_computation.59 | loop fusion | bytes 7864380 | tf_op jit(solution)/shard_map/dynamic_slice | solution.py:90
  10.7 6.0 %collective-permute-start = (bf16[256,512]{1,0:T(8,128)(2,1)}, bf16[256,512]{1,0:T(8,128)(2,1)}, u32[]{:S(2)}, u32[]{:S(2)}) collective-permute-start(bf16[256,512]{1,0:T(8,128)(2,1)} %get-tuple-element.7), channel_id=1, source_target_pairs={{0,7},{1,8},{2,9},{3,10},{4,11},{5,12},{6,13},{7,14},{8,15},{9,16}... | collective-permute-start | bytes 786440 | tf_op jit(solution)/shard_map/ppermute | solution.py:13
  16.7 4.1 %collective-permute-start.1 = (bf16[256,512]{1,0:T(8,128)(2,1)}, bf16[256,512]{1,0:T(8,128)(2,1)}, u32[]{:S(2)}, u32[]{:S(2)}) collective-permute-start(bf16[256,512]{1,0:T(8,128)(2,1)} %get-tuple-element.19), channel_id=1, source_target_pairs={{0,6},{1,7},{2,8},{3,9},{4,10},{5,11},{6,12},{7,13},{8,14},{9,15},... | collective-permute-start | bytes 786440 | tf_op jit(solution)/shard_map/ppermute | solution.py:13
  30.4 9.3 %all-to-all-start = ((bf16[4,32,2048]{2,0,1:T(4,128)(2,1)}), bf16[4,32,2048]{2,0,1:T(4,128)(2,1)}, u32[]{:S(2)}, u32[]{:S(2)}) async-start(bf16[4,32,2048]{2,0,1:T(4,128)(2,1)} %bitcast.67), calls=%async_computation | async-start | bytes 1048576 | tf_op jit(solution)/shard_map/all_to_all | solution.py:101
  41.1 4.0 %collective-permute-start.2 = (bf16[256,512]{1,0:T(8,128)(2,1)}, bf16[256,512]{1,0:T(8,128)(2,1)}, u32[]{:S(2)}, u32[]{:S(2)}) collective-permute-start(bf16[256,512]{1,0:T(8,128)(2,1)} %get-tuple-element.18), channel_id=1, source_target_pairs={{0,5},{1,6},{2,7},{3,8},{4,9},{5,10},{6,11},{7,12},{8,13},{9,14},{... | collective-permute-start | bytes 786440 | tf_op jit(solution)/shard_map/ppermute | solution.py:13
  45.2 6.2 %collective-permute-start.3 = (bf16[256,512]{1,0:T(8,128)(2,1)}, bf16[256,512]{1,0:T(8,128)(2,1)}, u32[]{:S(2)}, u32[]{:S(2)}) collective-permute-start(bf16[256,512]{1,0:T(8,128)(2,1)} %get-tuple-element.17), channel_id=1, source_target_pairs={{0,4},{1,5},{2,6},{3,7},{4,8},{5,9},{6,10},{7,11},{8,12},{9,13},{1... | collective-permute-start | bytes 786440 | tf_op jit(solution)/shard_map/ppermute | solution.py:13
  51.3 2.0 collective-permute-start.4
  53.6 4.2 %collective-permute-start.5 = (bf16[256,512]{1,0:T(8,128)(2,1)}, bf16[256,512]{1,0:T(8,128)(2,1)}, u32[]{:S(2)}, u32[]{:S(2)}) collective-permute-start(bf16[256,512]{1,0:T(8,128)(2,1)} %get-tuple-element.15), channel_id=1, source_target_pairs={{0,2},{1,3},{2,4},{3,5},{4,6},{5,7},{6,8},{7,9},{8,10},{9,11},{10,... | collective-permute-start | bytes 786440 | tf_op jit(solution)/shard_map/ppermute | solution.py:13
  57.9 2.0 %collective-permute-start.6 = (bf16[256,512]{1,0:T(8,128)(2,1)}, bf16[256,512]{1,0:T(8,128)(2,1)}, u32[]{:S(2)}, u32[]{:S(2)}) collective-permute-start(bf16[256,512]{1,0:T(8,128)(2,1)} %get-tuple-element.14), channel_id=1, source_target_pairs={{0,1},{1,2},{2,3},{3,4},{4,5},{5,6},{6,7},{7,8},{8,9},{9,10},{10,1... | collective-permute-start | bytes 786440 | tf_op jit(solution)/shard_map/ppermute | solution.py:13
  59.9 6.0 %collective-permute-done.2 = bf16[256,512]{1,0:T(8,128)(2,1)} collective-permute-done((bf16[256,512]{1,0:T(8,128)(2,1)}, bf16[256,512]{1,0:T(8,128)(2,1)}, u32[]{:S(2)}, u32[]{:S(2)}) %collective-permute-start.2) | collective-permute-done | bytes 262176 | tf_op jit(solution)/shard_map/ppermute | solution.py:13
  67.1 6.5 %collective-permute-done.3 = bf16[256,512]{1,0:T(8,128)(2,1)} collective-permute-done((bf16[256,512]{1,0:T(8,128)(2,1)}, bf16[256,512]{1,0:T(8,128)(2,1)}, u32[]{:S(2)}, u32[]{:S(2)}) %collective-permute-start.3) | collective-permute-done | bytes 262176 | tf_op jit(solution)/shard_map/ppermute | solution.py:13
  79.7 4.6 %collective-permute-done.8 = bf16[256,512]{1,0:T(8,128)(2,1)} collective-permute-done((bf16[256,512]{1,0:T(8,128)(2,1)}, bf16[256,512]{1,0:T(8,128)(2,1)}, u32[]{:S(2)}, u32[]{:S(2)}) %collective-permute-start.8) | collective-permute-done | bytes 262176 | tf_op jit(solution)/shard_map/ppermute | solution.py:13
  85.0 5.1 %select_select_fusion = bf16[8,256,512]{2,1,0:T(8,128)(2,1)} fusion(pred[8]{0:T(512)(128)(4,1)S(1)} %get-tuple-element.26, pred[8]{0:T(512)(128)(4,1)S(1)} %get-tuple-element.27, pred[8]{0:T(512)(128)(4,1)S(1)} %get-tuple-element.28, pred[8]{0:T(512)(128)(4,1)S(1)} %get-tuple-element.29, pred[8]{0:T(512)(128)(4,1)S(1)} %get-tuple-element.30, ...), kind=kLoop, calls=%fused_computation.9 | loop fusion | flops 15728640 | bytes 6029432 | tf_op jit(solution)/shard_map/jit(_where)/select_n | solution.py:94
  92.1 2.2 %fusion.7 = bf16[128,1,512]{2,0,1:T(8,128)(2,1)S(1)} fusion(bf16[128,2048]{1,0:T(8,128)(2,1)} %reshape.589, bf16[2048,512]{1,0:T(8,128)(2,1)} %bitcast.66), kind=kOutput, calls=%fused_computation.13 | convolution fusion | flops 268500992 | bytes 2752512 | tf_op jit(solution)/shard_map/dot_general | solution.py:105
  96.3 7.8 %all-to-all-start.1 = ((bf16[32,2,1024]{2,1,0:T(2,128)(2,1)}), bf16[32,2,1024]{2,1,0:T(2,128)(2,1)S(1)}, u32[]{:S(2)}, u32[]{:S(2)}) async-start(bf16[32,2,1024]{2,1,0:T(2,128)(2,1)} %reshape.604), calls=%async_computation.1 | async-start | bytes 262144 | tf_op jit(solution)/shard_map/all_to_all | solution.py:107
  106.3 6.0 %all-to-all-done.1 = bf16[32,2,1024]{2,1,0:T(2,128)(2,1)S(1)} async-done(((bf16[32,2,1024]{2,1,0:T(2,128)(2,1)}), bf16[32,2,1024]{2,1,0:T(2,128)(2,1)S(1)}, u32[]{:S(2)}, u32[]{:S(2)}) %all-to-all-start.1) | async-done | bytes 131104 | tf_op jit(solution)/shard_map/all_to_all | solution.py:107
  118.3 2.0 %reshape.591 = bf16[16,4,4096]{2,1,0:T(4,128)(2,1)} reshape(bf16[64,4096]{1,0:T(8,128)(2,1)} %convolution_convert_fusion.1) | data formatting | bytes 1048576 | tf_op jit(solution)/shard_map/reshape | solution.py:142
  120.3 19.7 %all_to_all.34 = bf16[16,4,4096]{2,1,0:T(4,128)(2,1)} all-to-all(bf16[16,4,4096]{2,1,0:T(4,128)(2,1)} %reshape.591), channel_id=1, replica_groups=mesh['groups'=1,'expert'=16,'replica'=2] {'expert'}, dimensions={0} | all-to-all | bytes 1048576 | tf_op jit(solution)/shard_map/all_to_all | solution.py:145
  142.0 2.8 %fusion.4 = f32[64,384]{1,0:T(8,128)S(1)} fusion(bf16[64,4096]{1,0:T(8,128)(2,1)} %reshape.592, bf16[1,4096,384]{2,1,0:T(8,128)(2,1)} %param.25), kind=kOutput, calls=%fused_computation.7 | convolution fusion | flops 201326592 | bytes 3768320 | tf_op jit(solution)/shard_map/dot_general | solution.py:149
  147.3 17.3 %all-reduce.2.cloned.1.call-done = bf16[16,4,4096]{2,0,1:T(8,128)(2,1)} async-done(((bf16[16,4,4096]{2,0,1:T(8,128)(2,1)}), bf16[16,4,4096]{2,0,1:T(8,128)(2,1)}) %all-reduce.2.cloned.1.call-update) | async-done | bytes 524304 | tf_op jit(solution)/shard_map/psum | solution.py:155
  164.6 2.2 %copy.34 = bf16[16,4,4096]{2,1,0:T(4,128)(2,1)} copy(bf16[16,4,4096]{2,0,1:T(8,128)(2,1)} %all-reduce.2.cloned.1.call-done) | data formatting | bytes 1048576 | tf_op jit(solution)/shard_map/psum | solution.py:155
  166.8 6.9 %all-to-all-start.3 = ((bf16[16,4,4096]{2,1,0:T(4,128)(2,1)}), bf16[16,4,4096]{2,1,0:T(4,128)(2,1)}, u32[]{:S(2)}, u32[]{:S(2)}) async-start(bf16[16,4,4096]{2,1,0:T(4,128)(2,1)} %copy.34), calls=%async_computation.3 | async-start | bytes 1048576 | tf_op jit(solution)/shard_map/all_to_all | solution.py:156
  173.7 15.5 %all-to-all-done.3 = bf16[16,4,4096]{2,1,0:T(4,128)(2,1)} async-done(((bf16[16,4,4096]{2,1,0:T(4,128)(2,1)}), bf16[16,4,4096]{2,1,0:T(4,128)(2,1)}, u32[]{:S(2)}, u32[]{:S(2)}) %all-to-all-start.3) | async-done | bytes 524320 | tf_op jit(solution)/shard_map/all_to_all | solution.py:156
  191.2 2.0 fusion
  (92 shorter events, 37.6 us)
Async XLA Ops:
  6.5 139.2 %copy-start = (bf16[1,384,4096]{2,1,0:T(8,128)(2,1)S(1)}, bf16[1,384,4096]{2,1,0:T(8,128)(2,1)}, u32[]{:S(2)}) copy-start(bf16[1,384,4096]{2,1,0:T(8,128)(2,1)} %param.27) | copy-start | bytes 9437188
  6.5 18.3 %copy-start.8 = (bf16[4,512]{1,0:T(4,128)(2,1)S(1)}, bf16[4,512]{1,0:T(4,128)(2,1)}, u32[]{:S(2)}) copy-start(bf16[4,512]{1,0:T(4,128)(2,1)} %param.15) | copy-start | bytes 12292
  6.5 21.1 %copy-start.9 = (bf16[4,512]{1,0:T(4,128)(2,1)S(1)}, bf16[4,512]{1,0:T(4,128)(2,1)}, u32[]{:S(2)}) copy-start(bf16[4,512]{1,0:T(4,128)(2,1)} %param.16) | copy-start | bytes 12292
  10.7 29.1 %collective-permute-start = (bf16[256,512]{1,0:T(8,128)(2,1)}, bf16[256,512]{1,0:T(8,128)(2,1)}, u32[]{:S(2)}, u32[]{:S(2)}) collective-permute-start(bf16[256,512]{1,0:T(8,128)(2,1)} %get-tuple-element.7), channel_id=1, source_target_pairs={{0,7},{1,8},{2,9},{3,10},{4,11},{5,12},{6,13},{7,14},{8,15},{9,16}... | collective-permute-start | bytes 786440 | tf_op jit(solution)/shard_map/ppermute | solution.py:13
  16.7 24.5 %collective-permute-start.1 = (bf16[256,512]{1,0:T(8,128)(2,1)}, bf16[256,512]{1,0:T(8,128)(2,1)}, u32[]{:S(2)}, u32[]{:S(2)}) collective-permute-start(bf16[256,512]{1,0:T(8,128)(2,1)} %get-tuple-element.19), channel_id=1, source_target_pairs={{0,6},{1,7},{2,8},{3,9},{4,10},{5,11},{6,12},{7,13},{8,14},{9,15},... | collective-permute-start | bytes 786440 | tf_op jit(solution)/shard_map/ppermute | solution.py:13
  20.8 24.4 %collective-permute-start.10 = (bf16[256,512]{1,0:T(8,128)(2,1)}, bf16[256,512]{1,0:T(8,128)(2,1)}, u32[]{:S(2)}, u32[]{:S(2)}) collective-permute-start(bf16[256,512]{1,0:T(8,128)(2,1)} %get-tuple-element.10), channel_id=1, source_target_pairs={{4,0},{5,1},{6,2},{7,3},{8,4},{9,5},{10,6},{11,7},{12,8},{13,9},{1... | collective-permute-start | bytes 786440 | tf_op jit(solution)/shard_map/ppermute | solution.py:13
  22.1 29.2 %collective-permute-start.11 = (bf16[256,512]{1,0:T(8,128)(2,1)}, bf16[256,512]{1,0:T(8,128)(2,1)}, u32[]{:S(2)}, u32[]{:S(2)}) collective-permute-start(bf16[256,512]{1,0:T(8,128)(2,1)} %get-tuple-element.9), channel_id=1, source_target_pairs={{5,0},{6,1},{7,2},{8,3},{9,4},{10,5},{11,6},{12,7},{13,8},{14,9},{... | collective-permute-start | bytes 786440 | tf_op jit(solution)/shard_map/ppermute | solution.py:13
  23.4 30.2 %collective-permute-start.12 = (bf16[256,512]{1,0:T(8,128)(2,1)}, bf16[256,512]{1,0:T(8,128)(2,1)}, u32[]{:S(2)}, u32[]{:S(2)}) collective-permute-start(bf16[256,512]{1,0:T(8,128)(2,1)} %get-tuple-element.8), channel_id=1, source_target_pairs={{6,0},{7,1},{8,2},{9,3},{10,4},{11,5},{12,6},{13,7},{14,8},{15,9},... | collective-permute-start | bytes 786440 | tf_op jit(solution)/shard_map/ppermute | solution.py:13
  27.7 25.7 %copy-start.6 = (s32[8,8]{1,0:T(8,128)S(1)}, s32[8,8]{1,0:T(8,128)}, u32[]{:S(2)}) copy-start(s32[8,8]{1,0:T(8,128)} %param.23) | copy-start | bytes 772
  30.4 59.6 %all-to-all-start = ((bf16[4,32,2048]{2,0,1:T(4,128)(2,1)}), bf16[4,32,2048]{2,0,1:T(4,128)(2,1)}, u32[]{:S(2)}, u32[]{:S(2)}) async-start(bf16[4,32,2048]{2,0,1:T(4,128)(2,1)} %bitcast.67), calls=%async_computation | async-start | bytes 1048576 | tf_op jit(solution)/shard_map/all_to_all | solution.py:101
  39.8 18.0 %collective-permute-start.13 = (bf16[256,512]{1,0:T(8,128)(2,1)}, bf16[256,512]{1,0:T(8,128)(2,1)}, u32[]{:S(2)}, u32[]{:S(2)}) collective-permute-start(bf16[256,512]{1,0:T(8,128)(2,1)} %get-tuple-element.21), channel_id=1, source_target_pairs={{7,0},{8,1},{9,2},{10,3},{11,4},{12,5},{13,6},{14,7},{15,8},{16,9}... | collective-permute-start | bytes 786440 | tf_op jit(solution)/shard_map/ppermute | solution.py:13
  41.1 24.7 %collective-permute-start.2 = (bf16[256,512]{1,0:T(8,128)(2,1)}, bf16[256,512]{1,0:T(8,128)(2,1)}, u32[]{:S(2)}, u32[]{:S(2)}) collective-permute-start(bf16[256,512]{1,0:T(8,128)(2,1)} %get-tuple-element.18), channel_id=1, source_target_pairs={{0,5},{1,6},{2,7},{3,8},{4,9},{5,10},{6,11},{7,12},{8,13},{9,14},{... | collective-permute-start | bytes 786440 | tf_op jit(solution)/shard_map/ppermute | solution.py:13
  45.2 28.4 %collective-permute-start.3 = (bf16[256,512]{1,0:T(8,128)(2,1)}, bf16[256,512]{1,0:T(8,128)(2,1)}, u32[]{:S(2)}, u32[]{:S(2)}) collective-permute-start(bf16[256,512]{1,0:T(8,128)(2,1)} %get-tuple-element.17), channel_id=1, source_target_pairs={{0,4},{1,5},{2,6},{3,7},{4,8},{5,9},{6,10},{7,11},{8,12},{9,13},{1... | collective-permute-start | bytes 786440 | tf_op jit(solution)/shard_map/ppermute | solution.py:13
  51.3 23.6 %collective-permute-start.4 = (bf16[256,512]{1,0:T(8,128)(2,1)}, bf16[256,512]{1,0:T(8,128)(2,1)}, u32[]{:S(2)}, u32[]{:S(2)}) collective-permute-start(bf16[256,512]{1,0:T(8,128)(2,1)} %get-tuple-element.16), channel_id=1, source_target_pairs={{0,3},{1,4},{2,5},{3,6},{4,7},{5,8},{6,9},{7,10},{8,11},{9,12},{10... | collective-permute-start | bytes 786440 | tf_op jit(solution)/shard_map/ppermute | solution.py:13
  53.6 26.0 %collective-permute-start.5 = (bf16[256,512]{1,0:T(8,128)(2,1)}, bf16[256,512]{1,0:T(8,128)(2,1)}, u32[]{:S(2)}, u32[]{:S(2)}) collective-permute-start(bf16[256,512]{1,0:T(8,128)(2,1)} %get-tuple-element.15), channel_id=1, source_target_pairs={{0,2},{1,3},{2,4},{3,5},{4,6},{5,7},{6,8},{7,9},{8,10},{9,11},{10,... | collective-permute-start | bytes 786440 | tf_op jit(solution)/shard_map/ppermute | solution.py:13
  57.9 21.8 %collective-permute-start.6 = (bf16[256,512]{1,0:T(8,128)(2,1)}, bf16[256,512]{1,0:T(8,128)(2,1)}, u32[]{:S(2)}, u32[]{:S(2)}) collective-permute-start(bf16[256,512]{1,0:T(8,128)(2,1)} %get-tuple-element.14), channel_id=1, source_target_pairs={{0,1},{1,2},{2,3},{3,4},{4,5},{5,6},{6,7},{7,8},{8,9},{9,10},{10,1... | collective-permute-start | bytes 786440 | tf_op jit(solution)/shard_map/ppermute | solution.py:13
  65.9 13.8 %collective-permute-start.7 = (bf16[256,512]{1,0:T(8,128)(2,1)}, bf16[256,512]{1,0:T(8,128)(2,1)}, u32[]{:S(2)}, u32[]{:S(2)}) collective-permute-start(bf16[256,512]{1,0:T(8,128)(2,1)} %get-tuple-element.13), channel_id=1, source_target_pairs={{1,0},{2,1},{3,2},{4,3},{5,4},{6,5},{7,6},{8,7},{9,8},{10,9},{11,1... | collective-permute-start | bytes 786440 | tf_op jit(solution)/shard_map/ppermute | solution.py:13
  73.6 10.6 %collective-permute-start.8 = (bf16[256,512]{1,0:T(8,128)(2,1)}, bf16[256,512]{1,0:T(8,128)(2,1)}, u32[]{:S(2)}, u32[]{:S(2)}) collective-permute-start(bf16[256,512]{1,0:T(8,128)(2,1)} %get-tuple-element.12), channel_id=1, source_target_pairs={{2,0},{3,1},{4,2},{5,3},{6,4},{7,5},{8,6},{9,7},{10,8},{11,9},{12,... | collective-permute-start | bytes 786440 | tf_op jit(solution)/shard_map/ppermute | solution.py:13
  74.9 10.1 %collective-permute-start.9 = (bf16[256,512]{1,0:T(8,128)(2,1)}, bf16[256,512]{1,0:T(8,128)(2,1)}, u32[]{:S(2)}, u32[]{:S(2)}) collective-permute-start(bf16[256,512]{1,0:T(8,128)(2,1)} %get-tuple-element.11), channel_id=1, source_target_pairs={{3,0},{4,1},{5,2},{6,3},{7,4},{8,5},{9,6},{10,7},{11,8},{12,9},{13... | collective-permute-start | bytes 786440 | tf_op jit(solution)/shard_map/ppermute | solution.py:13
  96.3 16.1 %all-to-all-start.1 = ((bf16[32,2,1024]{2,1,0:T(2,128)(2,1)}), bf16[32,2,1024]{2,1,0:T(2,128)(2,1)S(1)}, u32[]{:S(2)}, u32[]{:S(2)}) async-start(bf16[32,2,1024]{2,1,0:T(2,128)(2,1)} %reshape.604), calls=%async_computation.1 | async-start | bytes 262144 | tf_op jit(solution)/shard_map/all_to_all | solution.py:107
  104.1 60.5 %all-reduce.2.cloned.1.call-start = ((), (), s32[]{:S(2)}) async-start(), calls=%async_computation.4 | async-start | bytes 1048576 | tf_op jit(solution)/shard_map/psum | solution.py:155
  147.2 44.0 %copy-start.4 = (bf16[4,4096]{1,0:T(4,128)(2,1)S(1)}, bf16[4,4096]{1,0:T(4,128)(2,1)}, u32[]{:S(2)}) copy-start(bf16[4,4096]{1,0:T(4,128)(2,1)} %param.20) | copy-start | bytes 98308
  147.2 44.0 %copy-start.7 = (f32[64,8]{0,1:T(8,128)S(1)}, f32[64,8]{0,1:T(8,128)}, u32[]{:S(2)}) copy-start(f32[64,8]{0,1:T(8,128)} %get-tuple-element.5) | copy-start | bytes 6148
  166.8 22.4 %all-to-all-start.3 = ((bf16[16,4,4096]{2,1,0:T(4,128)(2,1)}), bf16[16,4,4096]{2,1,0:T(4,128)(2,1)}, u32[]{:S(2)}, u32[]{:S(2)}) async-start(bf16[16,4,4096]{2,1,0:T(4,128)(2,1)} %copy.34), calls=%async_computation.3 | async-start | bytes 1048576 | tf_op jit(solution)/shard_map/all_to_all | solution.py:156
  (5 other events, 43.0 us)
Sparse Core Ops, SparseCore 0:
  147.4 17.1 all-reduce.1
where the time goes:
time: 202 us; the launch traced here: 200 us
  starting transfers between devices  61.6 us (30%)
  waiting for transfers between devices  56.7 us (28%)
  blocking collectives  21.6 us (11%)
  local copies, waits for them, and re-layouts  18.3 us (9%)
  matrix products  14.3 us (7%)
  other arithmetic  13.8 us (7%)
  between operations  13.8 us (7%)
    ppermute x14, starting transfers between devices, shifted(): return lax.ppermute(block, axis, route)  37.6 us
    all_to_all x1, blocking collectives, on_device(): lax.all_to_all(outgoing, 'expert', split_axis=0, concat_axis=0, tiled=True)  19.7 us
    ppermute x14, waiting for transfers between devices, shifted(): return lax.ppermute(block, axis, route)  17.8 us
    psum x1, waiting for transfers between devices, on_device(): lax.psum(partial_value.astype(jnp.bfloat16), 'replica').astype(jnp.float32)  17.3 us
    all_to_all x1, waiting for transfers between devices, on_device(): lax.all_to_all(summed_halves.astype(jnp.bfloat16), 'expert', split_axis=0...  15.5 us
    all_to_all x1, starting transfers between devices, on_device(): lax.all_to_all(repeated, ('expert', 'replica'), split_axis=1, concat_axis...  9.28 us
    all_to_all x1, starting transfers between devices, on_device(): lax.all_to_all(partial_cols.astype(jnp.bfloat16), ('expert', 'replica'),...  7.84 us
    all_to_all x1, starting transfers between devices, on_device(): lax.all_to_all(summed_halves.astype(jnp.bfloat16), 'expert', split_axis=0...  6.88 us
  transfers between devices with their start and end apart: 18, of which 7 were waited for; matrix products, arithmetic and copies ran while one was open for 8% of the time, Pallas kernels for 0%

commit v1 on v0

--- a/solution.py
+++ b/solution.py
@@ -152,7 +152,9 @@
     partial_value = jnp.dot(hidden_act, w_down[0], preferred_element_type=jnp.float32).reshape(
         lead_shape + (model_width,)
     )
-    summed_halves = lax.psum(partial_value.astype(jnp.bfloat16), "replica").astype(jnp.float32)
+    summed_halves = jnp.sum(
+        lax.all_gather(partial_value.astype(jnp.bfloat16), "replica"), 0
+    ).astype(jnp.float32)
     arrived = lax.all_to_all(
         summed_halves.astype(jnp.bfloat16), "expert", split_axis=0, concat_axis=0, tiled=True
     ).astype(summed_halves.dtype)

time: 202 us -> 194 us (0.960)
  waiting for transfers between devices: 56.7 us -> 47.1 us
  other arithmetic: 13.8 us -> 16.2 us
    psum x1 -> x0, waiting for transfers between devices: 17.3 us -> none  [on_device(): lax.psum(partial_value.astype(jnp.bfloat16), 'replica').astype(jnp.float32)]
    all_gather x0 -> x1, waiting for transfers between devices: none -> 7.72 us  [on_device(): lax.all_gather(partial_value.astype(jnp.bfloat16), 'replica')]
    reduce_sum x0 -> x1, other arithmetic: none -> 2.37 us  [on_device(): jnp.sum(lax.all_gather(partial_value.astype(jnp.bfloat16), 'replica'), 0)]
    psum x1 -> x0, local copies, waits for them, and re-layouts: 2.25 us -> none  [on_device(): lax.psum(partial_value.astype(jnp.bfloat16), 'replica').astype(jnp.float32)]
    reduce_sum x0 -> x1, local copies, waits for them, and re-layouts: none -> 2.25 us  [on_device(): jnp.sum(lax.all_gather(partial_value.astype(jnp.bfloat16), 'replica'), 0)]
where the time goes in v1:
time: 194 us; the launch traced here: 193 us
  starting transfers between devices  61.6 us (32%)
  waiting for transfers between devices  47.1 us (24%)
  blocking collectives  21.6 us (11%)
  local copies, waits for them, and re-layouts  18.3 us (9%)
  other arithmetic  16.2 us (8%)
  matrix products  14.3 us (7%)
  between operations  13.8 us (7%)
    ppermute x14, starting transfers between devices, shifted(): return lax.ppermute(block, axis, route)  37.6 us
    all_to_all x1, blocking collectives, on_device(): lax.all_to_all(outgoing, 'expert', split_axis=0, concat_axis=0, tiled=True)  19.7 us
    ppermute x14, waiting for transfers between devices, shifted(): return lax.ppermute(block, axis, route)  17.8 us
    all_to_all x1, waiting for transfers between devices, on_device(): lax.all_to_all(summed_halves.astype(jnp.bfloat16), 'expert', split_axis=0...  15.5 us
    all_to_all x1, starting transfers between devices, on_device(): lax.all_to_all(repeated, ('expert', 'replica'), split_axis=1, concat_axis...  9.28 us
    all_to_all x1, starting transfers between devices, on_device(): lax.all_to_all(partial_cols.astype(jnp.bfloat16), ('expert', 'replica'),...  7.84 us
    all_gather x1, waiting for transfers between devices, on_device(): lax.all_gather(partial_value.astype(jnp.bfloat16), 'replica')  7.72 us
    all_to_all x1, starting transfers between devices, on_device(): lax.all_to_all(summed_halves.astype(jnp.bfloat16), 'expert', split_axis=0...  6.84 us
  transfers between devices with their start and end apart: 18, of which 7 were waited for; matrix products, arithmetic and copies ran while one was open for 8% of the time, Pallas kernels for 0%

profile of v1, /device:TPU:0, one launch (start us, length us, event | category | flops | bytes accessed | tf_op | source)
XLA Modules:
  0.0 192.8 jit_solution(16555486169572360408)
XLA Ops:
  6.6 4.1 %constant_dynamic-slice_fusion.15 = (bf16[256,512]{1,0:T(8,128)(2,1)}, bf16[256,512]{1,0:T(8,128)(2,1)}, bf16[256,512]{1,0:T(8,128)(2,1)}, bf16[256,512]{1,0:T(8...) fusion(bf16[256,4096]{1,0:T(8,128)(2,1)} %param.21, ...), kind=kLoop, calls=%fused_computation.59 | loop fusion | bytes 7864380 | tf_op jit(solution)/shard_map/dynamic_slice | solution.py:90
  10.7 6.0 %collective-permute-start = (bf16[256,512]{1,0:T(8,128)(2,1)}, bf16[256,512]{1,0:T(8,128)(2,1)}, u32[]{:S(2)}, u32[]{:S(2)}) collective-permute-start(bf16[256,512]{1,0:T(8,128)(2,1)} %get-tuple-element.7), channel_id=1, source_target_pairs={{0,7},{1,8},{2,9},{3,10},{4,11},{5,12},{6,13},{7,14},{8,15},{9,16}... | collective-permute-start | bytes 786440 | tf_op jit(solution)/shard_map/ppermute | solution.py:13
  16.7 4.1 %collective-permute-start.1 = (bf16[256,512]{1,0:T(8,128)(2,1)}, bf16[256,512]{1,0:T(8,128)(2,1)}, u32[]{:S(2)}, u32[]{:S(2)}) collective-permute-start(bf16[256,512]{1,0:T(8,128)(2,1)} %get-tuple-element.19), channel_id=1, source_target_pairs={{0,6},{1,7},{2,8},{3,9},{4,10},{5,11},{6,12},{7,13},{8,14},{9,15},... | collective-permute-start | bytes 786440 | tf_op jit(solution)/shard_map/ppermute | solution.py:13
  30.4 9.3 %all-to-all-start = ((bf16[4,32,2048]{2,0,1:T(4,128)(2,1)}), bf16[4,32,2048]{2,0,1:T(4,128)(2,1)}, u32[]{:S(2)}, u32[]{:S(2)}) async-start(bf16[4,32,2048]{2,0,1:T(4,128)(2,1)} %bitcast.68), calls=%async_computation | async-start | bytes 1048576 | tf_op jit(solution)/shard_map/all_to_all | solution.py:101
  41.1 4.0 %collective-permute-start.2 = (bf16[256,512]{1,0:T(8,128)(2,1)}, bf16[256,512]{1,0:T(8,128)(2,1)}, u32[]{:S(2)}, u32[]{:S(2)}) collective-permute-start(bf16[256,512]{1,0:T(8,128)(2,1)} %get-tuple-element.18), channel_id=1, source_target_pairs={{0,5},{1,6},{2,7},{3,8},{4,9},{5,10},{6,11},{7,12},{8,13},{9,14},{... | collective-permute-start | bytes 786440 | tf_op jit(solution)/shard_map/ppermute | solution.py:13
  45.2 6.2 %collective-permute-start.3 = (bf16[256,512]{1,0:T(8,128)(2,1)}, bf16[256,512]{1,0:T(8,128)(2,1)}, u32[]{:S(2)}, u32[]{:S(2)}) collective-permute-start(bf16[256,512]{1,0:T(8,128)(2,1)} %get-tuple-element.17), channel_id=1, source_target_pairs={{0,4},{1,5},{2,6},{3,7},{4,8},{5,9},{6,10},{7,11},{8,12},{9,13},{1... | collective-permute-start | bytes 786440 | tf_op jit(solution)/shard_map/ppermute | solution.py:13
  51.3 2.0 %collective-permute-start.4 = (bf16[256,512]{1,0:T(8,128)(2,1)}, bf16[256,512]{1,0:T(8,128)(2,1)}, u32[]{:S(2)}, u32[]{:S(2)}) collective-permute-start(bf16[256,512]{1,0:T(8,128)(2,1)} %get-tuple-element.16), channel_id=1, source_target_pairs={{0,3},{1,4},{2,5},{3,6},{4,7},{5,8},{6,9},{7,10},{8,11},{9,12},{10... | collective-permute-start | bytes 786440 | tf_op jit(solution)/shard_map/ppermute | solution.py:13
  53.6 4.2 %collective-permute-start.5 = (bf16[256,512]{1,0:T(8,128)(2,1)}, bf16[256,512]{1,0:T(8,128)(2,1)}, u32[]{:S(2)}, u32[]{:S(2)}) collective-permute-start(bf16[256,512]{1,0:T(8,128)(2,1)} %get-tuple-element.15), channel_id=1, source_target_pairs={{0,2},{1,3},{2,4},{3,5},{4,6},{5,7},{6,8},{7,9},{8,10},{9,11},{10,... | collective-permute-start | bytes 786440 | tf_op jit(solution)/shard_map/ppermute | solution.py:13
  57.9 2.0 %collective-permute-start.6 = (bf16[256,512]{1,0:T(8,128)(2,1)}, bf16[256,512]{1,0:T(8,128)(2,1)}, u32[]{:S(2)}, u32[]{:S(2)}) collective-permute-start(bf16[256,512]{1,0:T(8,128)(2,1)} %get-tuple-element.14), channel_id=1, source_target_pairs={{0,1},{1,2},{2,3},{3,4},{4,5},{5,6},{6,7},{7,8},{8,9},{9,10},{10,1... | collective-permute-start | bytes 786440 | tf_op jit(solution)/shard_map/ppermute | solution.py:13
  59.9 6.0 %collective-permute-done.2 = bf16[256,512]{1,0:T(8,128)(2,1)} collective-permute-done((bf16[256,512]{1,0:T(8,128)(2,1)}, bf16[256,512]{1,0:T(8,128)(2,1)}, u32[]{:S(2)}, u32[]{:S(2)}) %collective-permute-start.2) | collective-permute-done | bytes 262176 | tf_op jit(solution)/shard_map/ppermute | solution.py:13
  67.1 6.5 %collective-permute-done.3 = bf16[256,512]{1,0:T(8,128)(2,1)} collective-permute-done((bf16[256,512]{1,0:T(8,128)(2,1)}, bf16[256,512]{1,0:T(8,128)(2,1)}, u32[]{:S(2)}, u32[]{:S(2)}) %collective-permute-start.3) | collective-permute-done | bytes 262176 | tf_op jit(solution)/shard_map/ppermute | solution.py:13
  79.7 4.6 %collective-permute-done.8 = bf16[256,512]{1,0:T(8,128)(2,1)} collective-permute-done((bf16[256,512]{1,0:T(8,128)(2,1)}, bf16[256,512]{1,0:T(8,128)(2,1)}, u32[]{:S(2)}, u32[]{:S(2)}) %collective-permute-start.8) | collective-permute-done | bytes 262176 | tf_op jit(solution)/shard_map/ppermute | solution.py:13
  85.0 5.1 %select_select_fusion = bf16[8,256,512]{2,1,0:T(8,128)(2,1)} fusion(pred[8]{0:T(512)(128)(4,1)S(1)} %get-tuple-element.26, pred[8]{0:T(512)(128)(4,1)S(1)} %get-tuple-element.27, pred[8]{0:T(512)(128)(4,1)S(1)} %get-tuple-element.28, pred[8]{0:T(512)(128)(4,1)S(1)} %get-tuple-element.29, pred[8]{0:T(512)(128)(4,1)S(1)} %get-tuple-element.30, ...), kind=kLoop, calls=%fused_computation.9 | loop fusion | flops 15728640 | bytes 6029432 | tf_op jit(solution)/shard_map/jit(_where)/select_n | solution.py:94
  92.1 2.2 %fusion.7 = bf16[128,1,512]{2,0,1:T(8,128)(2,1)S(1)} fusion(bf16[128,2048]{1,0:T(8,128)(2,1)} %reshape.589, bf16[2048,512]{1,0:T(8,128)(2,1)} %bitcast.67), kind=kOutput, calls=%fused_computation.13 | convolution fusion | flops 268500992 | bytes 2752512 | tf_op jit(solution)/shard_map/dot_general | solution.py:105
  96.3 7.8 %all-to-all-start.1 = ((bf16[32,2,1024]{2,1,0:T(2,128)(2,1)}), bf16[32,2,1024]{2,1,0:T(2,128)(2,1)S(1)}, u32[]{:S(2)}, u32[]{:S(2)}) async-start(bf16[32,2,1024]{2,1,0:T(2,128)(2,1)} %reshape.605), calls=%async_computation.1 | async-start | bytes 262144 | tf_op jit(solution)/shard_map/all_to_all | solution.py:107
  106.3 6.0 %all-to-all-done.1 = bf16[32,2,1024]{2,1,0:T(2,128)(2,1)S(1)} async-done(((bf16[32,2,1024]{2,1,0:T(2,128)(2,1)}), bf16[32,2,1024]{2,1,0:T(2,128)(2,1)S(1)}, u32[]{:S(2)}, u32[]{:S(2)}) %all-to-all-start.1) | async-done | bytes 131104 | tf_op jit(solution)/shard_map/all_to_all | solution.py:107
  118.3 2.0 %reshape.591 = bf16[16,4,4096]{2,1,0:T(4,128)(2,1)} reshape(bf16[64,4096]{1,0:T(8,128)(2,1)} %convolution_convert_fusion.1) | data formatting | bytes 1048576 | tf_op jit(solution)/shard_map/reshape | solution.py:142
  120.3 19.7 %all_to_all.34 = bf16[16,4,4096]{2,1,0:T(4,128)(2,1)} all-to-all(bf16[16,4,4096]{2,1,0:T(4,128)(2,1)} %reshape.591), channel_id=1, replica_groups=mesh['groups'=1,'expert'=16,'replica'=2] {'expert'}, dimensions={0} | all-to-all | bytes 1048576 | tf_op jit(solution)/shard_map/all_to_all | solution.py:145
  142.0 2.8 %fusion.4 = f32[64,384]{1,0:T(8,128)S(1)} fusion(bf16[64,4096]{1,0:T(8,128)(2,1)} %reshape.592, bf16[1,4096,384]{2,1,0:T(8,128)(2,1)} %param.25), kind=kOutput, calls=%fused_computation.7 | convolution fusion | flops 201326592 | bytes 3768320 | tf_op jit(solution)/shard_map/dot_general | solution.py:149
  147.3 7.7 %all-gather.4.cloned.1.call-done = bf16[32,4,4096]{2,0,1:T(8,128)(2,1)} async-done(((bf16[16,4,4096]{2,0,1:T(8,128)(2,1)}), bf16[32,4,4096]{2,0,1:T(8,128)(2,1)}) %all-gather.4.cloned.1.call-update) | async-done | bytes 1048592 | tf_op jit(solution)/shard_map/all_gather | solution.py:156
  155.0 2.4 %reduce_sum.85 = bf16[16,4,4096]{2,0,1:T(8,128)(2,1)} reduce(bf16[2,16,4,4096]{3,1,0,2:T(8,128)(2,1)} %bitcast.73, bf16[]{:T(256)} %constant.138.clone.1), dimensions={0}, to_apply=%region_8.9 | reduce | flops 262144 | bytes 1572866 | tf_op jit(solution)/shard_map/reduce_sum | solution.py:155
  157.4 2.2 %copy.44 = bf16[16,4,4096]{2,1,0:T(4,128)(2,1)} copy(bf16[16,4,4096]{2,0,1:T(8,128)(2,1)} %reduce_sum.85) | data formatting | bytes 1048576 | tf_op jit(solution)/shard_map/reduce_sum | solution.py:155
  159.6 6.8 %all-to-all-start.3 = ((bf16[16,4,4096]{2,1,0:T(4,128)(2,1)}), bf16[16,4,4096]{2,1,0:T(4,128)(2,1)}, u32[]{:S(2)}, u32[]{:S(2)}) async-start(bf16[16,4,4096]{2,1,0:T(4,128)(2,1)} %copy.44), calls=%async_computation.3 | async-start | bytes 1048576 | tf_op jit(solution)/shard_map/all_to_all | solution.py:158
  166.5 15.5 %all-to-all-done.3 = bf16[16,4,4096]{2,1,0:T(4,128)(2,1)} async-done(((bf16[16,4,4096]{2,1,0:T(4,128)(2,1)}), bf16[16,4,4096]{2,1,0:T(4,128)(2,1)}, u32[]{:S(2)}, u32[]{:S(2)}) %all-to-all-start.3) | async-done | bytes 524320 | tf_op jit(solution)/shard_map/all_to_all | solution.py:158
  (93 shorter events, 39.6 us)
Async XLA Ops:
  6.5 139.2 %copy-start = (bf16[1,384,4096]{2,1,0:T(8,128)(2,1)S(1)}, bf16[1,384,4096]{2,1,0:T(8,128)(2,1)}, u32[]{:S(2)}) copy-start(bf16[1,384,4096]{2,1,0:T(8,128)(2,1)} %param.27) | copy-start | bytes 9437188
  6.5 18.3 %copy-start.8 = (bf16[4,512]{1,0:T(4,128)(2,1)S(1)}, bf16[4,512]{1,0:T(4,128)(2,1)}, u32[]{:S(2)}) copy-start(bf16[4,512]{1,0:T(4,128)(2,1)} %param.15) | copy-start | bytes 12292
  6.5 21.1 %copy-start.9 = (bf16[4,512]{1,0:T(4,128)(2,1)S(1)}, bf16[4,512]{1,0:T(4,128)(2,1)}, u32[]{:S(2)}) copy-start(bf16[4,512]{1,0:T(4,128)(2,1)} %param.16) | copy-start | bytes 12292
  10.7 29.1 %collective-permute-start = (bf16[256,512]{1,0:T(8,128)(2,1)}, bf16[256,512]{1,0:T(8,128)(2,1)}, u32[]{:S(2)}, u32[]{:S(2)}) collective-permute-start(bf16[256,512]{1,0:T(8,128)(2,1)} %get-tuple-element.7), channel_id=1, source_target_pairs={{0,7},{1,8},{2,9},{3,10},{4,11},{5,12},{6,13},{7,14},{8,15},{9,16}... | collective-permute-start | bytes 786440 | tf_op jit(solution)/shard_map/ppermute | solution.py:13
  16.7 24.5 %collective-permute-start.1 = (bf16[256,512]{1,0:T(8,128)(2,1)}, bf16[256,512]{1,0:T(8,128)(2,1)}, u32[]{:S(2)}, u32[]{:S(2)}) collective-permute-start(bf16[256,512]{1,0:T(8,128)(2,1)} %get-tuple-element.19), channel_id=1, source_target_pairs={{0,6},{1,7},{2,8},{3,9},{4,10},{5,11},{6,12},{7,13},{8,14},{9,15},... | collective-permute-start | bytes 786440 | tf_op jit(solution)/shard_map/ppermute | solution.py:13
  20.8 24.4 %collective-permute-start.10 = (bf16[256,512]{1,0:T(8,128)(2,1)}, bf16[256,512]{1,0:T(8,128)(2,1)}, u32[]{:S(2)}, u32[]{:S(2)}) collective-permute-start(bf16[256,512]{1,0:T(8,128)(2,1)} %get-tuple-element.10), channel_id=1, source_target_pairs={{4,0},{5,1},{6,2},{7,3},{8,4},{9,5},{10,6},{11,7},{12,8},{13,9},{1... | collective-permute-start | bytes 786440 | tf_op jit(solution)/shard_map/ppermute | solution.py:13
  22.1 29.2 %collective-permute-start.11 = (bf16[256,512]{1,0:T(8,128)(2,1)}, bf16[256,512]{1,0:T(8,128)(2,1)}, u32[]{:S(2)}, u32[]{:S(2)}) collective-permute-start(bf16[256,512]{1,0:T(8,128)(2,1)} %get-tuple-element.9), channel_id=1, source_target_pairs={{5,0},{6,1},{7,2},{8,3},{9,4},{10,5},{11,6},{12,7},{13,8},{14,9},{... | collective-permute-start | bytes 786440 | tf_op jit(solution)/shard_map/ppermute | solution.py:13
  23.4 30.2 %collective-permute-start.12 = (bf16[256,512]{1,0:T(8,128)(2,1)}, bf16[256,512]{1,0:T(8,128)(2,1)}, u32[]{:S(2)}, u32[]{:S(2)}) collective-permute-start(bf16[256,512]{1,0:T(8,128)(2,1)} %get-tuple-element.8), channel_id=1, source_target_pairs={{6,0},{7,1},{8,2},{9,3},{10,4},{11,5},{12,6},{13,7},{14,8},{15,9},... | collective-permute-start | bytes 786440 | tf_op jit(solution)/shard_map/ppermute | solution.py:13
  27.7 25.7 %copy-start.6 = (s32[8,8]{1,0:T(8,128)S(1)}, s32[8,8]{1,0:T(8,128)}, u32[]{:S(2)}) copy-start(s32[8,8]{1,0:T(8,128)} %param.23) | copy-start | bytes 772
  30.4 59.6 %all-to-all-start = ((bf16[4,32,2048]{2,0,1:T(4,128)(2,1)}), bf16[4,32,2048]{2,0,1:T(4,128)(2,1)}, u32[]{:S(2)}, u32[]{:S(2)}) async-start(bf16[4,32,2048]{2,0,1:T(4,128)(2,1)} %bitcast.68), calls=%async_computation | async-start | bytes 1048576 | tf_op jit(solution)/shard_map/all_to_all | solution.py:101
  39.8 18.0 %collective-permute-start.13 = (bf16[256,512]{1,0:T(8,128)(2,1)}, bf16[256,512]{1,0:T(8,128)(2,1)}, u32[]{:S(2)}, u32[]{:S(2)}) collective-permute-start(bf16[256,512]{1,0:T(8,128)(2,1)} %get-tuple-element.21), channel_id=1, source_target_pairs={{7,0},{8,1},{9,2},{10,3},{11,4},{12,5},{13,6},{14,7},{15,8},{16,9}... | collective-permute-start | bytes 786440 | tf_op jit(solution)/shard_map/ppermute | solution.py:13
  41.1 24.7 %collective-permute-start.2 = (bf16[256,512]{1,0:T(8,128)(2,1)}, bf16[256,512]{1,0:T(8,128)(2,1)}, u32[]{:S(2)}, u32[]{:S(2)}) collective-permute-start(bf16[256,512]{1,0:T(8,128)(2,1)} %get-tuple-element.18), channel_id=1, source_target_pairs={{0,5},{1,6},{2,7},{3,8},{4,9},{5,10},{6,11},{7,12},{8,13},{9,14},{... | collective-permute-start | bytes 786440 | tf_op jit(solution)/shard_map/ppermute | solution.py:13
  45.2 28.4 %collective-permute-start.3 = (bf16[256,512]{1,0:T(8,128)(2,1)}, bf16[256,512]{1,0:T(8,128)(2,1)}, u32[]{:S(2)}, u32[]{:S(2)}) collective-permute-start(bf16[256,512]{1,0:T(8,128)(2,1)} %get-tuple-element.17), channel_id=1, source_target_pairs={{0,4},{1,5},{2,6},{3,7},{4,8},{5,9},{6,10},{7,11},{8,12},{9,13},{1... | collective-permute-start | bytes 786440 | tf_op jit(solution)/shard_map/ppermute | solution.py:13
  51.3 23.6 %collective-permute-start.4 = (bf16[256,512]{1,0:T(8,128)(2,1)}, bf16[256,512]{1,0:T(8,128)(2,1)}, u32[]{:S(2)}, u32[]{:S(2)}) collective-permute-start(bf16[256,512]{1,0:T(8,128)(2,1)} %get-tuple-element.16), channel_id=1, source_target_pairs={{0,3},{1,4},{2,5},{3,6},{4,7},{5,8},{6,9},{7,10},{8,11},{9,12},{10... | collective-permute-start | bytes 786440 | tf_op jit(solution)/shard_map/ppermute | solution.py:13
  53.6 26.0 %collective-permute-start.5 = (bf16[256,512]{1,0:T(8,128)(2,1)}, bf16[256,512]{1,0:T(8,128)(2,1)}, u32[]{:S(2)}, u32[]{:S(2)}) collective-permute-start(bf16[256,512]{1,0:T(8,128)(2,1)} %get-tuple-element.15), channel_id=1, source_target_pairs={{0,2},{1,3},{2,4},{3,5},{4,6},{5,7},{6,8},{7,9},{8,10},{9,11},{10,... | collective-permute-start | bytes 786440 | tf_op jit(solution)/shard_map/ppermute | solution.py:13
  57.9 21.8 %collective-permute-start.6 = (bf16[256,512]{1,0:T(8,128)(2,1)}, bf16[256,512]{1,0:T(8,128)(2,1)}, u32[]{:S(2)}, u32[]{:S(2)}) collective-permute-start(bf16[256,512]{1,0:T(8,128)(2,1)} %get-tuple-element.14), channel_id=1, source_target_pairs={{0,1},{1,2},{2,3},{3,4},{4,5},{5,6},{6,7},{7,8},{8,9},{9,10},{10,1... | collective-permute-start | bytes 786440 | tf_op jit(solution)/shard_map/ppermute | solution.py:13
  65.9 13.8 %collective-permute-start.7 = (bf16[256,512]{1,0:T(8,128)(2,1)}, bf16[256,512]{1,0:T(8,128)(2,1)}, u32[]{:S(2)}, u32[]{:S(2)}) collective-permute-start(bf16[256,512]{1,0:T(8,128)(2,1)} %get-tuple-element.13), channel_id=1, source_target_pairs={{1,0},{2,1},{3,2},{4,3},{5,4},{6,5},{7,6},{8,7},{9,8},{10,9},{11,1... | collective-permute-start | bytes 786440 | tf_op jit(solution)/shard_map/ppermute | solution.py:13
  73.6 10.6 %collective-permute-start.8 = (bf16[256,512]{1,0:T(8,128)(2,1)}, bf16[256,512]{1,0:T(8,128)(2,1)}, u32[]{:S(2)}, u32[]{:S(2)}) collective-permute-start(bf16[256,512]{1,0:T(8,128)(2,1)} %get-tuple-element.12), channel_id=1, source_target_pairs={{2,0},{3,1},{4,2},{5,3},{6,4},{7,5},{8,6},{9,7},{10,8},{11,9},{12,... | collective-permute-start | bytes 786440 | tf_op jit(solution)/shard_map/ppermute | solution.py:13
  74.9 10.1 %collective-permute-start.9 = (bf16[256,512]{1,0:T(8,128)(2,1)}, bf16[256,512]{1,0:T(8,128)(2,1)}, u32[]{:S(2)}, u32[]{:S(2)}) collective-permute-start(bf16[256,512]{1,0:T(8,128)(2,1)} %get-tuple-element.11), channel_id=1, source_target_pairs={{3,0},{4,1},{5,2},{6,3},{7,4},{8,5},{9,6},{10,7},{11,8},{12,9},{13... | collective-permute-start | bytes 786440 | tf_op jit(solution)/shard_map/ppermute | solution.py:13
  96.3 16.1 %all-to-all-start.1 = ((bf16[32,2,1024]{2,1,0:T(2,128)(2,1)}), bf16[32,2,1024]{2,1,0:T(2,128)(2,1)S(1)}, u32[]{:S(2)}, u32[]{:S(2)}) async-start(bf16[32,2,1024]{2,1,0:T(2,128)(2,1)} %reshape.605), calls=%async_computation.1 | async-start | bytes 262144 | tf_op jit(solution)/shard_map/all_to_all | solution.py:107
  104.1 50.9 %all-gather.4.cloned.1.call-start = ((), (), s32[]{:S(2)}) async-start(), calls=%async_computation.4 | async-start | bytes 1572864 | tf_op jit(solution)/shard_map/all_gather | solution.py:156
  155.0 29.0 %copy-start.4 = (bf16[4,4096]{1,0:T(4,128)(2,1)S(1)}, bf16[4,4096]{1,0:T(4,128)(2,1)}, u32[]{:S(2)}) copy-start(bf16[4,4096]{1,0:T(4,128)(2,1)} %param.20) | copy-start | bytes 98308
  155.0 29.0 %copy-start.7 = (f32[64,8]{0,1:T(8,128)S(1)}, f32[64,8]{0,1:T(8,128)}, u32[]{:S(2)}) copy-start(f32[64,8]{0,1:T(8,128)} %get-tuple-element.5) | copy-start | bytes 6148
  159.6 22.4 %all-to-all-start.3 = ((bf16[16,4,4096]{2,1,0:T(4,128)(2,1)}), bf16[16,4,4096]{2,1,0:T(4,128)(2,1)}, u32[]{:S(2)}, u32[]{:S(2)}) async-start(bf16[16,4,4096]{2,1,0:T(4,128)(2,1)} %copy.44), calls=%async_computation.3 | async-start | bytes 1048576 | tf_op jit(solution)/shard_map/all_to_all | solution.py:158
  (5 other events, 43.0 us)
Sparse Core Ops, SparseCore 0:
  147.4 7.5 all-gather.3
